TPU v7x, 32 devices: a whole 2x2x4 slice. The times are simulated.
32 devices in a mesh: hyp: 2 (over x), rows: 16 (over z, y, core).
Axes of the slice: x: 2, y: 2, z: 4, core: 2. Of those that a mesh axis runs over, the one named last changes fastest.
Arguments:
- offsets: float32 [2, 65536], P(None, 'rows'), may hold values from 0 to 1
- tile_cell: int32 [512], P('rows'), may hold values from 0 to 31, as said below
- probes: int32 [8, 65536], P(None, 'rows'), may hold values from 0 to 1
- target: float32 [65536], P('rows'), may hold values from -6 to 6
- lengthscale: float32 [2], P('hyp'), parts along dimension 0, may hold values from 0.5 to 1
- amplitude: float32 [2], P('hyp'), parts along dimension 0, may hold values from 0.02 to 0.08
- noise: float32 [2], P('hyp'), parts along dimension 0, may hold values from 0.1 to 0.4
Outputs:
- solutions: float32 [18, 65536], P('hyp', 'rows'), parts along dimension 0
- quadratic: float32 [18], P('hyp'), parts along dimension 0
There are 2 independent parts, one for each index of `hyp`. A program takes and returns all parts, laid end to end along the dimension named above; an argument that names none is the same for every part. Nothing has to cross between parts.
Inputs may be any that keep to these rules, and one draw needn't show every extreme that they name: `tile_cell`: each aligned block of 32 entries (one device's tiles) is a permutation of 0 to 31.
All inputs are finite; a program needn't handle non-finite values.
Results may differ from a plain program's by a relative error of at most 0.0003.
Values sent between devices are 32-bit elements; how exact they have to be, the bound alone decides.
A program may use at most 64 MiB of HBM per device.

v0:
```python
import functools

import jax
import jax.numpy as jnp
from jax import lax
from jax.experimental import pallas as pl
from jax.experimental.pallas import tpu as pltpu
from jax.sharding import PartitionSpec as P

TILE = 128
GX = 16
RHS = 9
PAD = 16
FAR = 1.0e3
TINY = 1.0e-30
MESH = pl.DeviceIdType.MESH
F32 = jnp.float32
BF16 = jnp.bfloat16


def kernel(
    n, rows, points,
    order, cell, length, amp_ref, noise_ref, off_in, probes_in, target_in,
    x_ref, q_ref,
    off, probes, target, tiles, pk, hv, vx, whi, wlo, ohi, olo, sc, cm, acc, mom, gathered,
    load_sem, halo_send, halo_recv, mom_send, mom_recv,
):
    me = lax.axis_index("rows")
    has = (me > 0, me < n - 1)
    row_lanes = GX * TILE
    reach = 3 * TILE
    amp = amp_ref[0]
    shift = amp + noise_ref[0]

    barrier = pltpu.get_barrier_semaphore()

    def greet(k, carry):
        pl.semaphore_signal(
            barrier, inc=1, device_id={"rows": lax.rem(me + k, n)}, device_id_type=MESH
        )
        return carry

    lax.fori_loop(1, n, greet, 0)
    loads = [
        pltpu.make_async_copy(source, held, load_sem.at[i])
        for i, (source, held) in enumerate(
            ((off_in, off), (probes_in, probes), (target_in, target))
        )
    ]
    for load in loads:
        load.start()
    vx[...] = jnp.zeros_like(vx)
    cm[...] = jnp.zeros_like(cm)
    for sr in range(rows + 2):
        for edge in (0, (GX + 1) * TILE):
            sc[0, sr, edge : edge + TILE, :] = jnp.full((TILE, TILE), FAR, F32)
            sc[1, sr, edge : edge + TILE, :] = jnp.full((TILE, TILE), FAR, F32)
    for load in loads:
        load.wait()

    for g in range(rows * GX):
        lanes = slice(g * TILE, (g + 1) * TILE)
        tiles[g] = jnp.concatenate(
            [
                2.0 * probes[:, lanes].astype(F32) - 1.0,
                target[:, lanes],
                off[:, lanes],
                jnp.zeros((PAD - RHS - 2, TILE), F32),
            ],
            axis=0,
        )
    for g in range(rows * GX):
        pk[0, :, g * TILE : (g + 1) * TILE] = tiles[order[g]]

    pl.semaphore_wait(barrier, n - 1)

    def halo_copy(k, side):
        first = 0 if side == 0 else (rows - 1) * row_lanes
        return pltpu.make_async_remote_copy(
            src_ref=pk.at[k, :, pl.ds(first, row_lanes)],
            dst_ref=hv.at[k, 1 - side],
            send_sem=halo_send.at[k, side],
            recv_sem=halo_recv.at[k, 1 - side],
            device_id={"rows": me - 1 if side == 0 else me + 1},
            device_id_type=MESH,
        )

    def send_halo(k):
        for side in range(2):
            @pl.when(has[side])
            def _(side=side):
                halo_copy(k, side).start()

    send_halo(0)

    inverse = 1.0 / jnp.full((1, TILE), length[0], F32)

    def place_columns(sr, values):
        cm[0:GX] = jnp.concatenate([v[0] for v in values], axis=0)
        cm[GX : 2 * GX] = jnp.concatenate([v[1] for v in values], axis=0)
        turned = cm[...].T
        for c in range(GX):
            at = slice((c + 1) * TILE, (c + 2) * TILE)
            sc[0, sr, at, :] = jnp.broadcast_to(turned[:, c : c + 1], (TILE, TILE))
            sc[1, sr, at, :] = jnp.broadcast_to(turned[:, GX + c : GX + c + 1], (TILE, TILE))

    for side, sr in ((0, 0), (1, rows + 1)):
        @pl.when(jnp.logical_not(has[side]))
        def _(sr=sr):
            sc[0, sr] = jnp.full((sc.shape[2], TILE), FAR, F32)
            sc[1, sr] = jnp.full((sc.shape[2], TILE), FAR, F32)

    def split(par, sr, at, value):
        high = value.astype(BF16)
        vx[par, sr, 0:PAD, at] = high
        vx[par, sr, PAD : 2 * PAD, at] = (value - high.astype(F32)).astype(BF16)

    own = pl.ds(TILE, row_lanes)
    for a in range(rows):
        base = a * row_lanes
        split(0, a + 1, own, pk[0, :, base : base + row_lanes])
        place_columns(
            a + 1,
            [
                (
                    (pk[0, RHS : RHS + 1, base + c * TILE : base + (c + 1) * TILE] + a) * inverse,
                    (pk[0, RHS + 1 : RHS + 2, base + c * TILE : base + (c + 1) * TILE] + c) * inverse,
                )
                for c in range(GX)
            ],
        )

    def build(high_ref, low_ref, a, c, sr, first):
        base = pl.multiple_of(a * row_lanes + c * TILE, TILE)
        here = pk[0, :, pl.ds(base, TILE)]
        tx = (here[RHS : RHS + 1] + a) * inverse
        ty = (here[RHS + 1 : RHS + 2] + c.astype(F32)) * inverse
        step = 64
        for part in range(reach // step):
            at = pl.ds(pl.multiple_of(c * TILE + part * step, step), step)
            dx = sc[0, sr, at, :] - tx
            dy = sc[1, sr, at, :] - ty
            square = dx * dx + dy * dy
            close = jnp.maximum(1.0 - square * lax.rsqrt(jnp.maximum(square, TINY)), 0.0)
            twice = close * close
            w = twice * twice * (5.0 - 4.0 * close)
            high = w.astype(BF16)
            to = pl.ds(first + part * step, step)
            high_ref[to, :] = high
            low_ref[to, :] = (w - high.astype(F32)).astype(BF16)

    def apply(v, high_ref, low_ref):
        high, low = (
            jnp.concatenate([held[t] for t in range(held.shape[0])], axis=1)
            for held in (high_ref, low_ref)
        )
        r = jnp.dot(v, high, preferred_element_type=F32)
        s = jnp.dot(v[:PAD], low, preferred_element_type=F32)
        return r[:PAD] + r[PAD:] + s

    pair = 2 * TILE
    zero = jnp.zeros((PAD, TILE), F32)
    moments = []
    for k in range(3):
        par = k % 2

        def inner(c, carry, k=k, par=par):
            if k == 0:
                for sr in range(1, rows + 1):
                    for a in range(rows):
                        build(whi.at[c, a], wlo.at[c, a], a, c, sr, (sr - 1) * reach)
            lanes = pl.ds(pl.multiple_of(c * TILE, TILE), reach)
            v = jnp.concatenate([vx[par, sr, :, lanes] for sr in range(1, rows + 1)], axis=1)
            part = apply(v, whi.at[c], wlo.at[c])
            for a in range(rows):
                at = pl.ds(pl.multiple_of(a * row_lanes + c * TILE, TILE), TILE)
                acc[:, at] = part[:, a * TILE : (a + 1) * TILE]
            return carry

        lax.fori_loop(0, GX, inner, 0, unroll=2 if k == 0 else 8)

        for side, sr in ((0, 0), (1, rows + 1)):
            @pl.when(has[side])
            def _(side=side, sr=sr, k=k, par=par):
                pltpu.make_async_remote_copy(
                    src_ref=pk.at[k, :, pl.ds(0, row_lanes)],
                    dst_ref=hv.at[k, side],
                    send_sem=halo_send.at[k, side],
                    recv_sem=halo_recv.at[k, side],
                    device_id={"rows": me - 1 if side == 0 else me + 1},
                    device_id_type=MESH,
                ).wait_recv()
                split(par, sr, own, hv[k, side])
                if k == 0:
                    place_columns(
                        sr,
                        [
                            (
                                (hv[0, side, RHS : RHS + 1, c * TILE : (c + 1) * TILE] + (sr - 1)) * inverse,
                                (hv[0, side, RHS + 1 : RHS + 2, c * TILE : (c + 1) * TILE] + c) * inverse,
                            )
                            for c in range(GX)
                        ],
                    )

        def outer(c, carry, k=k, par=par):
            first, cross, square = carry
            sources = pl.ds(pl.multiple_of(c * pair, pair), 2 * pair)
            for a in range(rows):
                at = pl.ds(pl.multiple_of(a * row_lanes + c * pair, pair), pair)
                total = acc[:, at]
                for side, sr, edge in ((0, 0, 0), (1, rows + 1, rows - 1)):
                    if a != edge:
                        continue
                    if k == 0:
                        for held in (ohi, olo):
                            held[side, c, 0, 3 * TILE :] = jnp.zeros((TILE, TILE), BF16)
                            held[side, c, 1, :TILE] = jnp.zeros((TILE, TILE), BF16)
                        for t in range(2):
                            build(
                                ohi.at[side, c, t], olo.at[side, c, t], a, 2 * c + t, sr, t * TILE
                            )
                    total = total + apply(
                        vx[par, sr, :, sources], ohi.at[side, c], olo.at[side, c]
                    )
                now = pk[k, :, at]
                later = amp * (total - now)
                if k == 0:
                    first = first + now * now
                cross = cross + now * later
                if k < 2:
                    square = square + later * later
                    pk[k + 1, :, at] = later
                    split(1 - par, a + 1, pl.ds(pl.multiple_of(c * pair + TILE, TILE), pair), later)
            return first, cross, square

        wide = jnp.zeros((PAD, pair), F32)
        first, cross, square = lax.fori_loop(0, GX // 2, outer, (wide, wide, wide), unroll=1 if k == 0 else 8)
        moments += ([first] if k == 0 else []) + [cross] + ([square] if k < 2 else [])
        if k < 2:
            send_halo(k + 1)

    lane = lax.broadcasted_iota(jnp.int32, (PAD, TILE), 1)
    packed = zero
    for i, part in enumerate(moments):
        packed = jnp.where(lane == i, jnp.sum(part, axis=1, keepdims=True), packed)
    mom[...] = packed
    gathered[me] = packed

    def mom_copy(k):
        peer = lax.rem(me + k, n)
        return pltpu.make_async_remote_copy(
            src_ref=mom,
            dst_ref=gathered.at[me],
            send_sem=mom_send.at[peer],
            recv_sem=mom_recv.at[me],
            device_id={"rows": peer},
            device_id_type=MESH,
        )

    def mom_start(k, carry):
        mom_copy(k).start()
        return carry

    lax.fori_loop(1, n, mom_start, 0)

    def mom_wait(k, carry):
        peer = lax.rem(me + k, n)
        pltpu.make_async_remote_copy(
            src_ref=mom,
            dst_ref=gathered.at[peer],
            send_sem=mom_send.at[peer],
            recv_sem=mom_recv.at[peer],
            device_id={"rows": peer},
            device_id_type=MESH,
        ).wait()
        return carry

    lax.fori_loop(1, n, mom_wait, 0)
    total = lax.fori_loop(0, n, lambda j, t: t + gathered[j], zero)

    m = [total[:, i : i + 1] for i in range(6)]
    a00, a01, a02 = (m[i + 1] + shift * m[i] for i in range(3))
    a11, a12 = (m[i + 1] + shift * m[i] for i in range(2, 4))
    a22 = m[5] + shift * m[4]
    l1 = a01 / a00
    l2 = a02 / a00
    b11 = a11 - l1 * a01
    b12 = a12 - l1 * a02
    b22 = a22 - l2 * a02
    g1 = m[1] - l1 * m[0]
    g2 = m[2] - l2 * m[0]
    fine1 = b11 > 1.0e-6 * a11
    safe1 = jnp.where(fine1, b11, 1.0)
    l3 = b12 / safe1
    d22 = b22 - l3 * b12
    fine2 = jnp.logical_and(fine1, d22 > 1.0e-6 * a22)
    c2 = jnp.where(fine2, (g2 - l3 * g1) / jnp.where(fine2, d22, 1.0), 0.0)
    c1 = jnp.where(fine1, (g1 - b12 * c2) / safe1, 0.0)
    c0 = (m[0] - a01 * c1 - a02 * c2) / a00
    values = (c0 * m[0] + c1 * m[1] + c2 * m[2]) / points
    sublane = lax.broadcasted_iota(jnp.int32, (PAD, TILE), 0)
    turned = jnp.sum(jnp.where(lane == sublane, values, 0.0), axis=0, keepdims=True)
    q_ref[...] = turned[:, :RHS]

    for g in range(rows * GX):
        at = slice(g * TILE, (g + 1) * TILE)
        tiles[g] = c0 * pk[0, :, at] + c1 * pk[1, :, at] + c2 * pk[2, :, at]
    for s in range(rows * GX):
        found = tiles[cell[s]]
        x_ref[:, s * TILE : (s + 1) * TILE] = found[:RHS]

    for k in range(3):
        for side in range(2):
            @pl.when(has[side])
            def _(k=k, side=side):
                halo_copy(k, side).wait_send()


def shards(n, offsets, tile_cell, probes, target, lengthscale, amplitude, noise):
    tiles = tile_cell.shape[0]
    rows = tiles // GX
    places = jnp.arange(tiles, dtype=jnp.int32)
    order = jnp.sum(
        jnp.where(tile_cell[None, :] == places[:, None], places[None, :], 0), axis=1
    ).astype(jnp.int32)
    local = tiles * TILE
    width = (GX + 2) * TILE
    smem = pl.BlockSpec(memory_space=pltpu.SMEM)
    vmem = pl.BlockSpec(memory_space=pltpu.VMEM)
    solutions, quadratic = pl.pallas_call(
        functools.partial(kernel, n, rows, float(local * n)),
        out_shape=(
            jax.ShapeDtypeStruct((RHS, local), F32),
            jax.ShapeDtypeStruct((1, RHS), F32),
        ),
        in_specs=[smem] * 5 + [pl.BlockSpec(memory_space=pl.ANY)] * 3,
        out_specs=(vmem, vmem),
        scratch_shapes=[
            pltpu.VMEM((2, local), F32),
            pltpu.VMEM((RHS - 1, local), jnp.int32),
            pltpu.VMEM((1, local), F32),
            pltpu.VMEM((tiles, PAD, TILE), F32),
            pltpu.VMEM((3, PAD, local), F32),
            pltpu.VMEM((3, 2, PAD, GX * TILE), F32),
            pltpu.VMEM((2, rows + 2, 2 * PAD, width), BF16),
            pltpu.VMEM((GX, rows, rows * 3 * TILE, TILE), BF16),
            pltpu.VMEM((GX, rows, rows * 3 * TILE, TILE), BF16),
            pltpu.VMEM((2, GX // 2, 2, 4 * TILE, TILE), BF16),
            pltpu.VMEM((2, GX // 2, 2, 4 * TILE, TILE), BF16),
            pltpu.VMEM((2, rows + 2, width, TILE), F32),
            pltpu.VMEM((TILE, TILE), F32),
            pltpu.VMEM((PAD, local), F32),
            pltpu.VMEM((PAD, TILE), F32),
            pltpu.VMEM((n, PAD, TILE), F32),
            pltpu.SemaphoreType.DMA((3,)),
            pltpu.SemaphoreType.DMA((3, 2)),
            pltpu.SemaphoreType.DMA((3, 2)),
            pltpu.SemaphoreType.DMA((n,)),
            pltpu.SemaphoreType.DMA((n,)),
        ],
        compiler_params=pltpu.CompilerParams(
            collective_id=0, has_side_effects=True, vmem_limit_bytes=58 * 1024 * 1024
        ),
        name="solve",
    )(order, tile_cell, lengthscale, amplitude, noise, offsets, probes, target[None, :])
    return solutions, quadratic.reshape(RHS)


def solution(mesh):
    return jax.shard_map(
        functools.partial(shards, mesh.shape["rows"]),
        mesh=mesh,
        in_specs=(
            P(None, "rows"),
            P("rows"),
            P(None, "rows"),
            P("rows"),
            P("hyp"),
            P("hyp"),
            P("hyp"),
        ),
        out_specs=(P("hyp", "rows"), P("hyp")),
        check_vma=False,
    )
```

profile of v0, /device:TPU:0, one launch (start us, length us, event | category | flops | bytes accessed | tf_op | source)
XLA Modules:
  0.0 52.1 jit_solution(3731514169165596611)
XLA Ops:
  2.6 0.0 copy-start
  2.6 0.6 %copy-done = s32[32]{0:T(128)S(1)} copy-done((s32[32]{0:T(128)S(1)}, s32[32]{0:T(128)}, u32[]{:S(2)}) %copy-start) | copy-done | bytes 152
  3.2 0.6 %select_reduce_fusion.order = s32[32]{0:T(128)} fusion(s32[32]{0:T(128)S(1)} %copy-done), kind=kLoop, calls=%fused_computation | loop fusion | flops 3040 | bytes 256 | tf_op jit(solution)/shard_map/reduce_sum | solution.py:324
  3.9 46.0 %solve.1 = (f32[9,4096]{1,0:T(8,128)}, f32[1,9]{1,0:T(1,128)}) custom-call(s32[32]{0:T(128)} %select_reduce_fusion.order, s32[32]{0:T(128)} %cell.1, f32[1]{0:T(128)S(6)} %copy.11.length, f32[1]{0:T(128)S(6)} %copy.12.amp_ref, f32[1]{0:T(128)S(6)} %copy.13.noise_ref, f32[2,4096]{1,0:T(2,128)} %off_in.1, s32[8,4096]{1,0:T(8,128)} %probes_in.1, f32[1,4096]{1,0:T(1,128)} %bitcast.2), custom_call_target="tpu_custom_call" | custom-call | tf_op jit(solution)/shard_map/solve/pallas_call | solution.py:331
  49.9 0.0 copy-start.1
  49.9 1.7 %copy.14 = f32[9,4096]{1,0:T(8,128)} copy(f32[9,4096]{1,0:T(8,128)} %get-tuple-element.8) | data formatting | bytes 294912
  51.6 0.0 copy-done.1
  51.6 0.5 copy.15
Async XLA Ops:
  2.6 0.7 %copy-start = (s32[32]{0:T(128)S(1)}, s32[32]{0:T(128)}, u32[]{:S(2)}) copy-start(s32[32]{0:T(128)} %cell.1) | copy-start | bytes 388
  49.9 1.7 %copy-start.1 = (f32[1,9]{1,0:T(1,128)S(1)}, f32[1,9]{1,0:T(1,128)}, u32[]{:S(2)}) copy-start(f32[1,9]{1,0:T(1,128)} %get-tuple-element.5) | copy-start | bytes 112
where the time goes:
time: 52.3 us; the launch traced here: 52.1 us
  Pallas kernels  46 us (88%)
  local copies, waits for them, and re-layouts  2.84 us (5%)
  between operations  2.59 us (5%)
  other arithmetic  0.63 us (1%)
    pallas_call x1, Pallas kernels, shards(): pl.pallas_call(functools.partial(kernel, n, rows, float(local * n)), out_...  46 us
    unnamed x6, local copies, waits for them, and re-layouts  2.84 us

commit v1 on v0

v1 whole, which is shorter than its diff:
```python
import functools

import jax
import jax.numpy as jnp
from jax import lax
from jax.experimental import pallas as pl
from jax.experimental.pallas import tpu as pltpu
from jax.sharding import PartitionSpec as P

TILE = 128
GX = 16
RHS = 9
PAD = 16
FAR = 1.0e3
SNAP = 12.0
NUDGE = 2.0**-21
MESH = pl.DeviceIdType.MESH
F32 = jnp.float32
BF16 = jnp.bfloat16


def snap(value):
    return (value + SNAP) - SNAP


def kernel(
    n, rows, points,
    cell, length, amp_ref, noise_ref, off_in, probes_in, target_in,
    x_ref, q_ref,
    off, probes, target, raw, vec, last, place, snapped, hvec, hlast, hplace,
    vx, vh, whi, wlo, ohi, olo, even, odd, acc, mom, gathered,
    powers, load_sem, halo_send, halo_recv, mom_send, mom_recv,
):
    tiles = rows * GX
    wide = rows * TILE
    me = lax.axis_index("rows")
    has = (me > 0, me < n - 1)
    amp = amp_ref[0]
    shift = amp + noise_ref[0]

    barrier = pltpu.get_barrier_semaphore()

    def greet(k, carry):
        pl.semaphore_signal(
            barrier, inc=1, device_id={"rows": lax.rem(me + k, n)}, device_id_type=MESH
        )
        return carry

    lax.fori_loop(1, n, greet, 0)
    loads = [
        pltpu.make_async_copy(source, held, load_sem.at[i])
        for i, (source, held) in enumerate(
            ((off_in, off), (probes_in, probes), (target_in, target))
        )
    ]
    for load in loads:
        load.start()

    for s in range(tiles):
        powers[s] = jnp.int32((1 << s) - ((1 << 32) if s == 31 else 0))
    words = [jnp.int32(0)] * (tiles - 1).bit_length()
    for s in range(tiles):
        bit = powers[cell[s]]
        words = [w | bit if (s >> b) & 1 else w for b, w in enumerate(words)]
    order = []
    for g in range(tiles):
        place_of = jnp.int32(0)
        for b, w in enumerate(words):
            one = lax.shift_right_logical(w, jnp.int32(g)) & 1
            place_of = place_of | lax.shift_left(one, jnp.int32(b))
        order.append(place_of)

    inverse = 1.0 / jnp.full((1, TILE), length[0], F32)
    step = snap(inverse)

    def split(value):
        high = value.astype(BF16)
        return jnp.concatenate([high, (value - high.astype(F32)).astype(BF16)], axis=0)

    for edge in (0, GX + 1):
        for par in range(2):
            vx[par, edge] = jnp.zeros((2 * PAD, wide), BF16)
        for side in range(2):
            vh[side, edge] = jnp.zeros((2 * PAD, TILE), BF16)
    for held in (whi, wlo):
        held[0, 0] = jnp.zeros((wide, wide), BF16)
        held[GX - 1, 2] = jnp.zeros((wide, wide), BF16)

    for load in loads:
        load.wait()

    for g in range(tiles):
        at = slice(g * TILE, (g + 1) * TILE)
        raw[g] = jnp.concatenate(
            [
                2.0 * probes[:, at].astype(F32) - 1.0,
                target[:, at],
                off[:, at],
                jnp.zeros((PAD - RHS - 2, TILE), F32),
            ],
            axis=0,
        )
    kept = lax.broadcasted_iota(jnp.int32, (PAD, TILE), 0) < RHS
    for c in range(GX):
        for a in range(rows):
            value = raw[order[a * GX + c]]
            where = value[RHS : RHS + 2]
            value = jnp.where(kept, value, 0.0)
            vec[0, c, a] = value
            last[0, a, c] = value[RHS - 1 : RHS]
            place[a, c] = where
            snapped[c, a] = snap(where * inverse)
            vx[0, c + 1, :, a * TILE : (a + 1) * TILE] = split(value)

    def copies(k, side):
        row = 0 if side == 0 else rows - 1
        pairs = [
            (vec.at[k, :, row, 0 : RHS - 1, :], hvec.at[k, 1 - side]),
            (last.at[k, row], hlast.at[k, 1 - side]),
        ]
        if k == 0:
            pairs.append((place.at[row], hplace.at[1 - side]))
        return [
            pltpu.make_async_remote_copy(
                src_ref=source,
                dst_ref=target_ref,
                send_sem=halo_send.at[k, side, i],
                recv_sem=halo_recv.at[k, 1 - side, i],
                device_id={"rows": me - 1 if side == 0 else me + 1},
                device_id_type=MESH,
            )
            for i, (source, target_ref) in enumerate(pairs)
        ]

    def sends(k):
        return (0, 1) if k < 2 else (0,)

    def send_halo(k):
        for side in sends(k):
            @pl.when(has[side])
            def _(side=side):
                for copy in copies(k, side):
                    copy.start()

    def receive_halo(k):
        for side in sends(k):
            @pl.when(has[1 - side])
            def _(side=side):
                for i, dst in enumerate((hvec.at[k, 1 - side], hlast.at[k, 1 - side], hplace.at[1 - side])):
                    if i < 2 or k == 0:
                        pltpu.make_async_remote_copy(
                            src_ref=dst,
                            dst_ref=dst,
                            send_sem=halo_send.at[k, side, i],
                            recv_sem=halo_recv.at[k, 1 - side, i],
                            device_id={"rows": me + 1 if side == 0 else me - 1},
                            device_id_type=MESH,
                        ).wait_recv()

            @pl.when(jnp.logical_not(has[1 - side]))
            def _(side=side):
                hvec[k, 1 - side] = jnp.zeros(hvec.shape[2:], F32)
                hlast[k, 1 - side] = jnp.zeros(hlast.shape[2:], F32)
                if k == 0:
                    hplace[1 - side] = jnp.full(hplace.shape[1:], FAR, F32)

            for c in range(GX):
                vh[1 - side, c + 1] = split(
                    jnp.concatenate(
                        [hvec[k, 1 - side, c], hlast[k, 1 - side, c], jnp.zeros((PAD - RHS, TILE), F32)],
                        axis=0,
                    )
                )

    def spread(held, where):
        for axis in range(2):
            held[axis] = jnp.broadcast_to(where[axis : axis + 1], (TILE, TILE)).T

    def weights(held, where, down, right):
        tx = where[0:1] + (down * step + NUDGE)
        ty = where[1:2] + right * step
        high, low = [], []
        size = 64
        for part in range(TILE // size):
            at = slice(part * size, (part + 1) * size)
            dx = held[0, at, :] - tx
            dy = held[1, at, :] - ty
            square = dx * dx + dy * dy
            close = jnp.maximum(1.0 - square * lax.rsqrt(square), 0.0)
            twice = close * close
            w = twice * twice * (1.25 - close)
            top = w.astype(BF16)
            high.append(top)
            low.append((w - top.astype(F32)).astype(BF16))
        return jnp.concatenate(high, axis=0), jnp.concatenate(low, axis=0)

    def put(c, j, source, to, pair):
        down = slice(source * TILE, (source + 1) * TILE)
        right = slice(to * TILE, (to + 1) * TILE)
        whi[c, j, down, right] = pair[0]
        wlo[c, j, down, right] = pair[1]

    def column(c, held, fresh, more=True):
        if more:
            for a in range(rows):
                spread(fresh.at[a], snapped[c + 1, a])
        for a in range(rows):
            for b in range(a, rows):
                pair = weights(held.at[a], snapped[c, b], b - a, 0)
                put(c, 1, a, b, pair)
                if b > a:
                    put(c, 1, b, a, tuple(p.T for p in pair))
        if more:
            for a in range(rows):
                for b in range(rows):
                    pair = weights(held.at[a], snapped[c + 1, b], b - a, 1)
                    put(c + 1, 0, a, b, pair)
                    put(c, 2, b, a, tuple(p.T for p in pair))

    def two(i, carry):
        column(2 * i, even, odd)
        column(2 * i + 1, odd, even)
        return carry

    for a in range(rows):
        spread(even.at[a], snapped[0, a])
    half = GX // 2 - 1
    lax.fori_loop(0, half - 3, two, 0)
    pl.semaphore_wait(barrier, n - 1)
    send_halo(0)
    lax.fori_loop(half - 3, half, two, 0)
    column(GX - 2, even, odd)
    column(GX - 1, odd, even, more=False)

    def apply(v, high, low):
        r = jnp.dot(v, high, preferred_element_type=F32)
        s = jnp.dot(v[:PAD], low, preferred_element_type=F32)
        return r[:PAD] + r[PAD:] + s

    def inner(par, count):
        def run(c, carry):
            v = [vx[par, c + j] for j in range(count)]
            if count < 3:
                v[1] = v[1] * BF16(0.5)
            high, low = (
                jnp.concatenate([held[c, j] for j in range(count)], axis=0)
                for held in (whi, wlo)
            )
            acc[c] = apply(jnp.concatenate(v, axis=1), high, low)
            return carry

        lax.fori_loop(0, GX, run, 0, unroll=8)

    def outer_weights(p, carry):
        for side in range(2):
            row = 0 if side == 0 else rows - 1
            down = 1 if side == 0 else -1
            for held in (ohi, olo):
                held[side, p + 1, 0, 3 * TILE :] = jnp.zeros((TILE, TILE), BF16)
                held[side, p + 1, 1, :TILE] = jnp.zeros((TILE, TILE), BF16)
            for t in range(2):
                c = 2 * p + t
                fresh = (even, odd)[side].at[t]
                spread(fresh, snap(hplace[side, c] * inverse))
                for move in (-1, 0, 1):
                    spot = t + move
                    to, slot = p + 1 + spot // 2, spot % 2
                    source = t + 1 - 2 * (spot // 2)
                    near = jnp.clip(c + move, 0, GX - 1)
                    high, low = weights(fresh, snapped[near, row], down, move)
                    down_at = slice(source * TILE, (source + 1) * TILE)
                    ohi[side, to, slot, down_at] = high
                    olo[side, to, slot, down_at] = low
        return carry

    def outer(k, par):
        def run(p, carry):
            first, cross, square = carry
            edges = {}
            for side in (0, 1) if k < 2 else (1,):
                v = jnp.concatenate([vh[side, 2 * p + j] for j in range(4)], axis=1)
                high, low = (
                    jnp.concatenate([held[side, p + 1, t] for t in range(2)], axis=1)
                    for held in (ohi, olo)
                )
                edges[side] = apply(v, high, low)
            for t in range(2):
                c = 2 * p + t
                for a in range(rows):
                    total = acc[c, :, a * TILE : (a + 1) * TILE]
                    for side, row in ((0, 0), (1, rows - 1)):
                        if a == row and side in edges:
                            total = total + edges[side][:, t * TILE : (t + 1) * TILE]
                    now = vec[k, c, a]
                    if k < 2:
                        later = (4.0 * amp) * total - amp * now
                        if k == 0:
                            first = first + now * now
                        cross = cross + now * later
                        square = square + later * later
                        vec[k + 1, c, a] = later
                        last[k + 1, a, c] = later[RHS - 1 : RHS]
                        vx[1 - par, c + 1, :, a * TILE : (a + 1) * TILE] = split(later)
                    else:
                        cross = cross + now * total
            return first, cross, square

        blank = jnp.zeros((PAD, TILE), F32)
        return lax.fori_loop(0, GX // 2, run, (blank, blank, blank), unroll=8)

    moments = []
    for k in range(3):
        par = k % 2
        inner(par, 3 if k < 2 else 2)
        receive_halo(k)
        if k == 0:
            lax.fori_loop(0, GX // 2, outer_weights, 0)
            for side in range(2):
                for held in (ohi, olo):
                    held[side, 1, 0, :TILE] = jnp.zeros((TILE, TILE), BF16)
                    held[side, GX // 2, 1, 3 * TILE :] = jnp.zeros((TILE, TILE), BF16)
        first, cross, square = outer(k, par)
        if k == 0:
            moments.append(first)
        if k < 2:
            moments += [cross, square]
            send_halo(k + 1)
        else:
            moments.append((8.0 * amp) * cross - amp * moments[4])

    lane = lax.broadcasted_iota(jnp.int32, (RHS - 1, TILE), 1)
    packed = jnp.zeros((RHS - 1, TILE), F32)
    for i, part in enumerate(moments):
        total = jnp.sum(part, axis=1, keepdims=True)
        packed = jnp.where(lane == i, total[: RHS - 1], packed)
        packed = jnp.where(lane == i + len(moments), total[RHS - 1 : RHS], packed)
    mom[...] = packed
    gathered[me] = packed

    def mom_copy(k):
        peer = lax.rem(me + k, n)
        return pltpu.make_async_remote_copy(
            src_ref=mom,
            dst_ref=gathered.at[me],
            send_sem=mom_send.at[peer],
            recv_sem=mom_recv.at[me],
            device_id={"rows": peer},
            device_id_type=MESH,
        )

    def mom_start(k, carry):
        mom_copy(k).start()
        return carry

    lax.fori_loop(1, n, mom_start, 0)

    def mom_wait(k, carry):
        peer = lax.rem(me + k, n)
        pltpu.make_async_remote_copy(
            src_ref=mom,
            dst_ref=gathered.at[peer],
            send_sem=mom_send.at[peer],
            recv_sem=mom_recv.at[peer],
            device_id={"rows": peer},
            device_id_type=MESH,
        ).wait()
        return carry

    lax.fori_loop(1, n, mom_wait, 0)
    total = lax.fori_loop(0, n, lambda j, t: t + gathered[j], jnp.zeros((RHS - 1, TILE), F32))

    m = [
        jnp.concatenate([total[:, i : i + 1], total[:, i + 6 : i + 7]], axis=0)
        for i in range(6)
    ]
    a00, a01, a02 = (m[i + 1] + shift * m[i] for i in range(3))
    a11, a12 = (m[i + 1] + shift * m[i] for i in range(2, 4))
    a22 = m[5] + shift * m[4]
    l1 = a01 / a00
    l2 = a02 / a00
    b11 = a11 - l1 * a01
    b12 = a12 - l1 * a02
    b22 = a22 - l2 * a02
    g1 = m[1] - l1 * m[0]
    g2 = m[2] - l2 * m[0]
    fine1 = b11 > 1.0e-6 * a11
    safe1 = jnp.where(fine1, b11, 1.0)
    l3 = b12 / safe1
    d22 = b22 - l3 * b12
    fine2 = jnp.logical_and(fine1, d22 > 1.0e-6 * a22)
    c2 = jnp.where(fine2, (g2 - l3 * g1) / jnp.where(fine2, d22, 1.0), 0.0)
    c1 = jnp.where(fine1, (g1 - b12 * c2) / safe1, 0.0)
    c0 = (m[0] - a01 * c1 - a02 * c2) / a00
    values = (c0 * m[0] + c1 * m[1] + c2 * m[2]) / points
    flat = lax.broadcasted_iota(jnp.int32, (PAD, TILE), 1)
    sublane = lax.broadcasted_iota(jnp.int32, (PAD, TILE), 0)
    turned = jnp.sum(jnp.where(flat == sublane, values, 0.0), axis=0, keepdims=True)
    q_ref[...] = turned[:, :RHS]

    c0, c1, c2 = (jnp.broadcast_to(c, (PAD, TILE)) for c in (c0, c1, c2))
    for s in range(tiles):
        spot = cell[s]
        a, c = spot // GX, spot % GX
        found = c0 * vec[0, c, a] + c1 * vec[1, c, a] + c2 * vec[2, c, a]
        x_ref[:, s * TILE : (s + 1) * TILE] = found[:RHS]

    for k in range(3):
        for side in sends(k):
            @pl.when(has[side])
            def _(k=k, side=side):
                for copy in copies(k, side):
                    copy.wait_send()


def shards(n, offsets, tile_cell, probes, target, lengthscale, amplitude, noise):
    tiles = tile_cell.shape[0]
    rows = tiles // GX
    local = tiles * TILE
    wide = rows * TILE
    smem = pl.BlockSpec(memory_space=pltpu.SMEM)
    vmem = pl.BlockSpec(memory_space=pltpu.VMEM)
    solutions, quadratic = pl.pallas_call(
        functools.partial(kernel, n, rows, float(local * n)),
        out_shape=(
            jax.ShapeDtypeStruct((RHS, local), F32),
            jax.ShapeDtypeStruct((1, RHS), F32),
        ),
        in_specs=[smem] * 4 + [pl.BlockSpec(memory_space=pl.ANY)] * 3,
        out_specs=(vmem, vmem),
        scratch_shapes=[
            pltpu.VMEM((2, local), F32),
            pltpu.VMEM((RHS - 1, local), jnp.int32),
            pltpu.VMEM((1, local), F32),
            pltpu.VMEM((tiles, PAD, TILE), F32),
            pltpu.VMEM((3, GX, rows, PAD, TILE), F32),
            pltpu.VMEM((3, rows, GX, 1, TILE), F32),
            pltpu.VMEM((rows, GX, 2, TILE), F32),
            pltpu.VMEM((GX, rows, 2, TILE), F32),
            pltpu.VMEM((3, 2, GX, RHS - 1, TILE), F32),
            pltpu.VMEM((3, 2, GX, 1, TILE), F32),
            pltpu.VMEM((2, GX, 2, TILE), F32),
            pltpu.VMEM((2, GX + 2, 2 * PAD, wide), BF16),
            pltpu.VMEM((2, GX + 2, 2 * PAD, TILE), BF16),
            pltpu.VMEM((GX, 3, wide, wide), BF16),
            pltpu.VMEM((GX, 3, wide, wide), BF16),
            pltpu.VMEM((2, GX // 2 + 2, 2, 4 * TILE, TILE), BF16),
            pltpu.VMEM((2, GX // 2 + 2, 2, 4 * TILE, TILE), BF16),
            pltpu.VMEM((rows, 2, TILE, TILE), F32),
            pltpu.VMEM((rows, 2, TILE, TILE), F32),
            pltpu.VMEM((GX, PAD, wide), F32),
            pltpu.VMEM((RHS - 1, TILE), F32),
            pltpu.VMEM((n, RHS - 1, TILE), F32),
            pltpu.SMEM((tiles,), jnp.int32),
            pltpu.SemaphoreType.DMA((3,)),
            pltpu.SemaphoreType.DMA((3, 2, 3)),
            pltpu.SemaphoreType.DMA((3, 2, 3)),
            pltpu.SemaphoreType.DMA((n,)),
            pltpu.SemaphoreType.DMA((n,)),
        ],
        compiler_params=pltpu.CompilerParams(
            collective_id=0, has_side_effects=True, vmem_limit_bytes=52 * 1024 * 1024
        ),
        name="solve",
    )(tile_cell, lengthscale, amplitude, noise, offsets, probes, target[None, :])
    return solutions, quadratic.reshape(RHS)


def solution(mesh):
    return jax.shard_map(
        functools.partial(shards, mesh.shape["rows"]),
        mesh=mesh,
        in_specs=(
            P(None, "rows"),
            P("rows"),
            P(None, "rows"),
            P("rows"),
            P("hyp"),
            P("hyp"),
            P("hyp"),
        ),
        out_specs=(P("hyp", "rows"), P("hyp")),
        check_vma=False,
    )
```

time: 52.3 us -> 37.8 us (0.72)
  Pallas kernels: 46 us -> 30.7 us
  local copies, waits for them, and re-layouts: 2.84 us -> 4.24 us
  other arithmetic: 0.63 us -> 0 us
    pallas_call x1, Pallas kernels: 46 us -> 30.7 us  [shards(): pl.pallas_call(functools.partial(kernel, n, rows, float(local * n)), out_...]
    unnamed x6 -> x10, local copies, waits for them, and re-layouts: 2.84 us -> 4.24 us
    reduce_sum x1 -> x0, other arithmetic: 0.63 us -> none  [shards(): jnp.sum(jnp.where(tile_cell[None, :] == places[:, None], places[None, :],...]
where the time goes in v1:
time: 37.8 us; the launch traced here: 37.5 us
  Pallas kernels  30.7 us (81%)
  local copies, waits for them, and re-layouts  4.24 us (11%)
  between operations  2.59 us (7%)
    pallas_call x1, Pallas kernels, shards(): pl.pallas_call(functools.partial(kernel, n, rows, float(local * n)), out_...  30.7 us
    unnamed x10, local copies, waits for them, and re-layouts  4.24 us

profile of v1, /device:TPU:0, one launch (start us, length us, event | category | flops | bytes accessed | tf_op | source)
XLA Modules:
  0.0 37.5 jit_solution(1651553923477479021)
XLA Ops:
  2.6 0.0 copy-start.3
  2.6 0.6 %copy-done.3 = s32[32]{0:T(128)S(1)} copy-done((s32[32]{0:T(128)S(1)}, s32[32]{0:T(128)}, u32[]{:S(2)}) %copy-start.3) | copy-done | bytes 152
  3.2 0.0 copy-start
  3.2 0.9 %copy-done = s32[8,4096]{1,0:T(8,128)S(1)} copy-done((s32[8,4096]{1,0:T(8,128)S(1)}, s32[8,4096]{1,0:T(8,128)}, u32[]{:S(2)}) %copy-start) | copy-done | bytes 131096
  4.1 0.0 copy-start.1
  4.1 0.8 %copy-done.1 = f32[2,4096]{1,0:T(2,128)S(1)} copy-done((f32[2,4096]{1,0:T(2,128)S(1)}, f32[2,4096]{1,0:T(2,128)}, u32[]{:S(2)}) %copy-start.1) | copy-done | bytes 32792
  4.9 0.0 copy-start.2
  4.9 0.7 %copy-done.2 = f32[4096]{0:T(1024)S(1)} copy-done((f32[4096]{0:T(1024)S(1)}, f32[4096]{0:T(1024)}, u32[]{:S(2)}) %copy-start.2) | copy-done | bytes 16408
  5.6 30.7 %solve.1 = (f32[9,4096]{1,0:T(8,128)S(1)}, f32[1,9]{1,0:T(1,128)S(1)}) custom-call(s32[32]{0:T(128)S(1)} %copy-done.3, f32[1]{0:T(128)S(6)} %copy.11.length, f32[1]{0:T(128)S(6)} %copy.12.amp_ref, f32[1]{0:T(128)S(6)} %copy.13.noise_ref, f32[2,4096]{1,0:T(2,128)S(1)} %copy-done.1, s32[8,4096]{1,0:T(8,128)S(1)} %copy-done, f32[1,4096]{1,0:T(1,128)S(1)} %bitcast.2), custom_call_target="tpu_custom_call" | custom-call | tf_op jit(solution)/shard_map/solve/pallas_call | solution.py:422
  36.3 0.7 %copy.14 = f32[9,4096]{1,0:T(8,128)} copy(f32[9,4096]{1,0:T(8,128)S(1)} %get-tuple-element.8) | data formatting | bytes 294912
  37.0 0.5 %copy.15 = f32[9]{0:T(128)} copy(f32[9]{0:T(128)S(1)} %bitcast.3) | data formatting | bytes 72
Async XLA Ops:
  2.6 0.7 %copy-start.3 = (s32[32]{0:T(128)S(1)}, s32[32]{0:T(128)}, u32[]{:S(2)}) copy-start(s32[32]{0:T(128)} %cell.1) | copy-start | bytes 388
  3.2 0.9 %copy-start = (s32[8,4096]{1,0:T(8,128)S(1)}, s32[8,4096]{1,0:T(8,128)}, u32[]{:S(2)}) copy-start(s32[8,4096]{1,0:T(8,128)} %probes_in.1) | copy-start | bytes 393220
  4.1 0.8 %copy-start.1 = (f32[2,4096]{1,0:T(2,128)S(1)}, f32[2,4096]{1,0:T(2,128)}, u32[]{:S(2)}) copy-start(f32[2,4096]{1,0:T(2,128)} %off_in.1) | copy-start | bytes 98308
  4.9 0.7 %copy-start.2 = (f32[4096]{0:T(1024)S(1)}, f32[4096]{0:T(1024)}, u32[]{:S(2)}) copy-start(f32[4096]{0:T(1024)} %param.10) | copy-start | bytes 49156

commit v2 on v1

--- a/solution.py
+++ b/solution.py
@@ -12,11 +12,14 @@
 RHS = 9
 PAD = 16
 FAR = 1.0e3
-SNAP = 12.0
-NUDGE = 2.0**-21
+SCALE = 8.0
+SNAP = 12.0 * SCALE
+NUDGE = SCALE * 2.0**-21
+GAIN = 4.0 / SCALE**5
 MESH = pl.DeviceIdType.MESH
 F32 = jnp.float32
 BF16 = jnp.bfloat16
+F8 = jnp.float8_e4m3fn
 
 
 def snap(value):
@@ -25,9 +28,9 @@
 
 def kernel(
     n, rows, points,
-    cell, length, amp_ref, noise_ref, off_in, probes_in, target_in,
+    cell_in, off_in, probes_in, target_in, length, amp_ref, noise_ref,
     x_ref, q_ref,
-    off, probes, target, raw, vec, last, place, snapped, hvec, hlast, hplace,
+    cell, off, probes, target, raw, vec, last, place, snapped, hvec, hlast, hplace,
     vx, vh, whi, wlo, ohi, olo, even, odd, acc, mom, gathered,
     powers, load_sem, halo_send, halo_recv, mom_send, mom_recv,
 ):
@@ -35,8 +38,6 @@
     wide = rows * TILE
     me = lax.axis_index("rows")
     has = (me > 0, me < n - 1)
-    amp = amp_ref[0]
-    shift = amp + noise_ref[0]
 
     barrier = pltpu.get_barrier_semaphore()
 
@@ -46,15 +47,20 @@
         )
         return carry
 
-    lax.fori_loop(1, n, greet, 0)
     loads = [
         pltpu.make_async_copy(source, held, load_sem.at[i])
         for i, (source, held) in enumerate(
-            ((off_in, off), (probes_in, probes), (target_in, target))
+            (
+                (cell_in, cell), (off_in, off), (probes_in, probes), (target_in, target),
+            )
         )
     ]
     for load in loads:
         load.start()
+    lax.fori_loop(1, n, greet, 0)
+    loads[0].wait()
+    amp = amp_ref[0]
+    shift = amp + noise_ref[0]
 
     for s in range(tiles):
         powers[s] = jnp.int32((1 << s) - ((1 << 32) if s == 31 else 0))
@@ -70,7 +76,7 @@
             place_of = place_of | lax.shift_left(one, jnp.int32(b))
         order.append(place_of)
 
-    inverse = 1.0 / jnp.full((1, TILE), length[0], F32)
+    inverse = SCALE / jnp.full((1, TILE), length[0], F32)
     step = snap(inverse)
 
     def split(value):
@@ -83,10 +89,10 @@
         for side in range(2):
             vh[side, edge] = jnp.zeros((2 * PAD, TILE), BF16)
     for held in (whi, wlo):
-        held[0, 0] = jnp.zeros((wide, wide), BF16)
-        held[GX - 1, 2] = jnp.zeros((wide, wide), BF16)
-
-    for load in loads:
+        held[0, 0] = jnp.zeros((wide, wide), held.dtype)
+        held[GX - 1, 2] = jnp.zeros((wide, wide), held.dtype)
+
+    for load in loads[1:]:
         load.wait()
 
     for g in range(tiles):
@@ -186,12 +192,12 @@
             dx = held[0, at, :] - tx
             dy = held[1, at, :] - ty
             square = dx * dx + dy * dy
-            close = jnp.maximum(1.0 - square * lax.rsqrt(square), 0.0)
+            close = jnp.maximum(SCALE - square * lax.rsqrt(square), 0.0)
             twice = close * close
-            w = twice * twice * (1.25 - close)
+            w = twice * twice * (1.25 * SCALE - close)
             top = w.astype(BF16)
             high.append(top)
-            low.append((w - top.astype(F32)).astype(BF16))
+            low.append((w - top.astype(F32)).astype(F8))
         return jnp.concatenate(high, axis=0), jnp.concatenate(low, axis=0)
 
     def put(c, j, source, to, pair):
@@ -225,10 +231,10 @@
     for a in range(rows):
         spread(even.at[a], snapped[0, a])
     half = GX // 2 - 1
-    lax.fori_loop(0, half - 3, two, 0)
+    lax.fori_loop(0, half - 5, two, 0)
     pl.semaphore_wait(barrier, n - 1)
     send_halo(0)
-    lax.fori_loop(half - 3, half, two, 0)
+    lax.fori_loop(half - 5, half, two, 0)
     column(GX - 2, even, odd)
     column(GX - 1, odd, even, more=False)
 
@@ -237,7 +243,7 @@
         s = jnp.dot(v[:PAD], low, preferred_element_type=F32)
         return r[:PAD] + r[PAD:] + s
 
-    def inner(par, count):
+    def inner_run(par, count):
         def run(c, carry):
             v = [vx[par, c + j] for j in range(count)]
             if count < 3:
@@ -249,15 +255,20 @@
             acc[c] = apply(jnp.concatenate(v, axis=1), high, low)
             return carry
 
-        lax.fori_loop(0, GX, run, 0, unroll=8)
+        return run
+
+    def inner(par, count):
+        lax.fori_loop(0, GX, inner_run(par, count), 0, unroll=16)
 
     def outer_weights(p, carry):
+        inner_run(0, 3)(2 * p, 0)
+        inner_run(0, 3)(2 * p + 1, 0)
         for side in range(2):
             row = 0 if side == 0 else rows - 1
             down = 1 if side == 0 else -1
             for held in (ohi, olo):
-                held[side, p + 1, 0, 3 * TILE :] = jnp.zeros((TILE, TILE), BF16)
-                held[side, p + 1, 1, :TILE] = jnp.zeros((TILE, TILE), BF16)
+                held[side, p + 1, 0, 3 * TILE :] = jnp.zeros((TILE, TILE), held.dtype)
+                held[side, p + 1, 1, :TILE] = jnp.zeros((TILE, TILE), held.dtype)
             for t in range(2):
                 c = 2 * p + t
                 fresh = (even, odd)[side].at[t]
@@ -293,7 +304,7 @@
                             total = total + edges[side][:, t * TILE : (t + 1) * TILE]
                     now = vec[k, c, a]
                     if k < 2:
-                        later = (4.0 * amp) * total - amp * now
+                        later = (GAIN * amp) * total - amp * now
                         if k == 0:
                             first = first + now * now
                         cross = cross + now * later
@@ -311,14 +322,15 @@
     moments = []
     for k in range(3):
         par = k % 2
-        inner(par, 3 if k < 2 else 2)
+        if k > 0:
+            inner(par, 3 if k < 2 else 2)
         receive_halo(k)
         if k == 0:
             lax.fori_loop(0, GX // 2, outer_weights, 0)
             for side in range(2):
                 for held in (ohi, olo):
-                    held[side, 1, 0, :TILE] = jnp.zeros((TILE, TILE), BF16)
-                    held[side, GX // 2, 1, 3 * TILE :] = jnp.zeros((TILE, TILE), BF16)
+                    held[side, 1, 0, :TILE] = jnp.zeros((TILE, TILE), held.dtype)
+                    held[side, GX // 2, 1, 3 * TILE :] = jnp.zeros((TILE, TILE), held.dtype)
         first, cross, square = outer(k, par)
         if k == 0:
             moments.append(first)
@@ -326,7 +338,7 @@
             moments += [cross, square]
             send_halo(k + 1)
         else:
-            moments.append((8.0 * amp) * cross - amp * moments[4])
+            moments.append((2.0 * GAIN * amp) * cross - amp * moments[4])
 
     lane = lax.broadcasted_iota(jnp.int32, (RHS - 1, TILE), 1)
     packed = jnp.zeros((RHS - 1, TILE), F32)
@@ -417,7 +429,6 @@
     rows = tiles // GX
     local = tiles * TILE
     wide = rows * TILE
-    smem = pl.BlockSpec(memory_space=pltpu.SMEM)
     vmem = pl.BlockSpec(memory_space=pltpu.VMEM)
     solutions, quadratic = pl.pallas_call(
         functools.partial(kernel, n, rows, float(local * n)),
@@ -425,9 +436,11 @@
             jax.ShapeDtypeStruct((RHS, local), F32),
             jax.ShapeDtypeStruct((1, RHS), F32),
         ),
-        in_specs=[smem] * 4 + [pl.BlockSpec(memory_space=pl.ANY)] * 3,
+        in_specs=[pl.BlockSpec(memory_space=pltpu.HBM)] * 4
+        + [pl.BlockSpec(memory_space=pltpu.SMEM)] * 3,
         out_specs=(vmem, vmem),
         scratch_shapes=[
+            pltpu.SMEM((tiles,), jnp.int32),
             pltpu.VMEM((2, local), F32),
             pltpu.VMEM((RHS - 1, local), jnp.int32),
             pltpu.VMEM((1, local), F32),
@@ -442,16 +455,16 @@
             pltpu.VMEM((2, GX + 2, 2 * PAD, wide), BF16),
             pltpu.VMEM((2, GX + 2, 2 * PAD, TILE), BF16),
             pltpu.VMEM((GX, 3, wide, wide), BF16),
-            pltpu.VMEM((GX, 3, wide, wide), BF16),
+            pltpu.VMEM((GX, 3, wide, wide), F8),
             pltpu.VMEM((2, GX // 2 + 2, 2, 4 * TILE, TILE), BF16),
-            pltpu.VMEM((2, GX // 2 + 2, 2, 4 * TILE, TILE), BF16),
+            pltpu.VMEM((2, GX // 2 + 2, 2, 4 * TILE, TILE), F8),
             pltpu.VMEM((rows, 2, TILE, TILE), F32),
             pltpu.VMEM((rows, 2, TILE, TILE), F32),
             pltpu.VMEM((GX, PAD, wide), F32),
             pltpu.VMEM((RHS - 1, TILE), F32),
             pltpu.VMEM((n, RHS - 1, TILE), F32),
             pltpu.SMEM((tiles,), jnp.int32),
-            pltpu.SemaphoreType.DMA((3,)),
+            pltpu.SemaphoreType.DMA((4,)),
             pltpu.SemaphoreType.DMA((3, 2, 3)),
             pltpu.SemaphoreType.DMA((3, 2, 3)),
             pltpu.SemaphoreType.DMA((n,)),
@@ -461,7 +474,15 @@
             collective_id=0, has_side_effects=True, vmem_limit_bytes=52 * 1024 * 1024
         ),
         name="solve",
-    )(tile_cell, lengthscale, amplitude, noise, offsets, probes, target[None, :])
+    )(
+        *(
+            pltpu.with_memory_space_constraint(x, pltpu.HBM)
+            for x in (tile_cell, offsets, probes, target[None, :])
+        ),
+        lengthscale,
+        amplitude,
+        noise,
+    )
     return solutions, quadratic.reshape(RHS)
 
 

time: 37.8 us -> 31.9 us (0.84)
  local copies, waits for them, and re-layouts: 4.24 us -> 1.22 us
  Pallas kernels: 30.7 us -> 27.9 us
    unnamed x10 -> x2, local copies, waits for them, and re-layouts: 4.24 us -> 1.22 us
    pallas_call x1, Pallas kernels: 30.7 us -> 27.9 us  [shards(): pl.pallas_call(functools.partial(kernel, n, rows, float(local * n)), out_...]
where the time goes in v2:
time: 31.9 us; the launch traced here: 31.7 us
  Pallas kernels  27.9 us (87%)
  between operations  2.58 us (8%)
  local copies, waits for them, and re-layouts  1.22 us (4%)
    pallas_call x1, Pallas kernels, shards(): pl.pallas_call(functools.partial(kernel, n, rows, float(local * n)), out_...  27.9 us
    unnamed x2, local copies, waits for them, and re-layouts  1.22 us

profile of v2, /device:TPU:0, one launch (start us, length us, event | category | flops | bytes accessed | tf_op | source)
XLA Modules:
  0.0 31.7 jit_solution(9799142892688173096)
XLA Ops:
  2.6 27.9 %solve.1 = (f32[9,4096]{1,0:T(8,128)S(1)}, f32[1,9]{1,0:T(1,128)S(1)}) custom-call(s32[32]{0:T(128)} %cell_in.1, f32[2,4096]{1,0:T(2,128)} %off_in.1, s32[8,4096]{1,0:T(8,128)} %probes_in.1, f32[1,4096]{1,0:T(1,128)} %bitcast.3, f32[1]{0:T(128)S(6)} %copy.11.length, f32[1]{0:T(128)S(6)} %copy.12.amp_ref, f32[1]{0:T(128)S(6)} %copy.13.noise_ref), custom_call_target="tpu_custom_call" | custom-call | tf_op jit(solution)/shard_map/solve/pallas_call | solution.py:433
  30.5 0.7 %copy.14 = f32[9,4096]{1,0:T(8,128)} copy(f32[9,4096]{1,0:T(8,128)S(1)} %get-tuple-element.8) | data formatting | bytes 294912
  31.2 0.5 %copy.15 = f32[9]{0:T(128)} copy(f32[9]{0:T(128)S(1)} %bitcast.2) | data formatting | bytes 72

commit v3 on v2

--- a/solution.py
+++ b/solution.py
@@ -9,6 +9,7 @@
 
 TILE = 128
 GX = 16
+CUT = 8
 RHS = 9
 PAD = 16
 FAR = 1.0e3
@@ -30,7 +31,7 @@
     n, rows, points,
     cell_in, off_in, probes_in, target_in, length, amp_ref, noise_ref,
     x_ref, q_ref,
-    cell, off, probes, target, raw, vec, last, place, snapped, hvec, hlast, hplace,
+    cell, off, probes, target, raw, vec, snapped, outbox, inbox, hsnap,
     vx, vh, whi, wlo, ohi, olo, even, odd, acc, mom, gathered,
     powers, load_sem, halo_send, halo_recv, mom_send, mom_recv,
 ):
@@ -94,6 +95,12 @@
 
     for load in loads[1:]:
         load.wait()
+
+    def pack(k, a, part, spot, value):
+        for side, row in ((0, 0), (1, rows - 1)):
+            if a == row:
+                outbox[k, side, part, spot] = value[: RHS - 1]
+                outbox[k, side, part, CUT, pl.ds(spot, 1)] = value[RHS - 1 : RHS]
 
     for g in range(tiles):
         at = slice(g * TILE, (g + 1) * TILE)
@@ -113,70 +120,75 @@
             where = value[RHS : RHS + 2]
             value = jnp.where(kept, value, 0.0)
             vec[0, c, a] = value
-            last[0, a, c] = value[RHS - 1 : RHS]
-            place[a, c] = where
+            pack(0, a, c // CUT, c % CUT, value)
+            for side, row in ((0, 0), (1, rows - 1)):
+                if a == row:
+                    for axis in range(2):
+                        outbox[0, side, c // CUT, CUT + 1 + axis, c % CUT : c % CUT + 1] = where[axis : axis + 1]
             snapped[c, a] = snap(where * inverse)
             vx[0, c + 1, :, a * TILE : (a + 1) * TILE] = split(value)
 
-    def copies(k, side):
-        row = 0 if side == 0 else rows - 1
-        pairs = [
-            (vec.at[k, :, row, 0 : RHS - 1, :], hvec.at[k, 1 - side]),
-            (last.at[k, row], hlast.at[k, 1 - side]),
-        ]
-        if k == 0:
-            pairs.append((place.at[row], hplace.at[1 - side]))
-        return [
-            pltpu.make_async_remote_copy(
-                src_ref=source,
-                dst_ref=target_ref,
-                send_sem=halo_send.at[k, side, i],
-                recv_sem=halo_recv.at[k, 1 - side, i],
-                device_id={"rows": me - 1 if side == 0 else me + 1},
-                device_id_type=MESH,
-            )
-            for i, (source, target_ref) in enumerate(pairs)
-        ]
+    def copy(k, side, part):
+        tiles_sent = CUT + (3 if k == 0 else 1)
+        return pltpu.make_async_remote_copy(
+            src_ref=outbox.at[k, side, part, 0:tiles_sent],
+            dst_ref=inbox.at[k, 1 - side, part, 0:tiles_sent],
+            send_sem=halo_send.at[k, side, part],
+            recv_sem=halo_recv.at[k, 1 - side, part],
+            device_id={"rows": me - 1 if side == 0 else me + 1},
+            device_id_type=MESH,
+        )
 
     def sends(k):
         return (0, 1) if k < 2 else (0,)
 
-    def send_halo(k):
+    def send_halo(k, part):
         for side in sends(k):
             @pl.when(has[side])
             def _(side=side):
-                for copy in copies(k, side):
-                    copy.start()
+                copy(k, side, part).start()
 
     def receive_halo(k):
         for side in sends(k):
             @pl.when(has[1 - side])
             def _(side=side):
-                for i, dst in enumerate((hvec.at[k, 1 - side], hlast.at[k, 1 - side], hplace.at[1 - side])):
-                    if i < 2 or k == 0:
-                        pltpu.make_async_remote_copy(
-                            src_ref=dst,
-                            dst_ref=dst,
-                            send_sem=halo_send.at[k, side, i],
-                            recv_sem=halo_recv.at[k, 1 - side, i],
-                            device_id={"rows": me + 1 if side == 0 else me - 1},
-                            device_id_type=MESH,
-                        ).wait_recv()
+                for part in range(2):
+                    landed = inbox.at[k, 1 - side, part, 0 : CUT + (3 if k == 0 else 1)]
+                    pltpu.make_async_remote_copy(
+                        src_ref=landed,
+                        dst_ref=landed,
+                        send_sem=halo_send.at[k, side, part],
+                        recv_sem=halo_recv.at[k, 1 - side, part],
+                        device_id={"rows": me + 1 if side == 0 else me - 1},
+                        device_id_type=MESH,
+                    ).wait_recv()
 
             @pl.when(jnp.logical_not(has[1 - side]))
             def _(side=side):
-                hvec[k, 1 - side] = jnp.zeros(hvec.shape[2:], F32)
-                hlast[k, 1 - side] = jnp.zeros(hlast.shape[2:], F32)
+                inbox[k, 1 - side] = jnp.zeros(inbox.shape[2:], F32)
                 if k == 0:
-                    hplace[1 - side] = jnp.full(hplace.shape[1:], FAR, F32)
+                    for part in range(2):
+                        inbox[0, 1 - side, part, CUT + 1 :] = jnp.full((2, CUT, TILE), FAR, F32)
 
             for c in range(GX):
+                part, spot = c // CUT, c % CUT
+                row = slice(spot, spot + 1)
                 vh[1 - side, c + 1] = split(
                     jnp.concatenate(
-                        [hvec[k, 1 - side, c], hlast[k, 1 - side, c], jnp.zeros((PAD - RHS, TILE), F32)],
+                        [
+                            inbox[k, 1 - side, part, spot],
+                            inbox[k, 1 - side, part, CUT, row],
+                            jnp.zeros((PAD - RHS, TILE), F32),
+                        ],
                         axis=0,
                     )
                 )
+                if k == 0:
+                    where = jnp.concatenate(
+                        [inbox[0, 1 - side, part, CUT + 1 + axis, row] for axis in range(2)],
+                        axis=0,
+                    )
+                    hsnap[1 - side, c] = snap(where * inverse)
 
     def spread(held, where):
         for axis in range(2):
@@ -233,7 +245,8 @@
     half = GX // 2 - 1
     lax.fori_loop(0, half - 5, two, 0)
     pl.semaphore_wait(barrier, n - 1)
-    send_halo(0)
+    send_halo(0, 0)
+    send_halo(0, 1)
     lax.fori_loop(half - 5, half, two, 0)
     column(GX - 2, even, odd)
     column(GX - 1, odd, even, more=False)
@@ -272,7 +285,7 @@
             for t in range(2):
                 c = 2 * p + t
                 fresh = (even, odd)[side].at[t]
-                spread(fresh, snap(hplace[side, c] * inverse))
+                spread(fresh, hsnap[side, c])
                 for move in (-1, 0, 1):
                     spot = t + move
                     to, slot = p + 1 + spot // 2, spot % 2
@@ -310,33 +323,52 @@
                         cross = cross + now * later
                         square = square + later * later
                         vec[k + 1, c, a] = later
-                        last[k + 1, a, c] = later[RHS - 1 : RHS]
+                        pack(k + 1, a, c // CUT, c % CUT, later)
                         vx[1 - par, c + 1, :, a * TILE : (a + 1) * TILE] = split(later)
                     else:
                         cross = cross + now * total
             return first, cross, square
 
-        blank = jnp.zeros((PAD, TILE), F32)
-        return lax.fori_loop(0, GX // 2, run, (blank, blank, blank), unroll=8)
-
+        return run
+
+    blank = jnp.zeros((PAD, TILE), F32)
+    pairs = GX // 2
     moments = []
     for k in range(3):
         par = k % 2
         if k > 0:
             inner(par, 3 if k < 2 else 2)
         receive_halo(k)
+        run = outer(k, par)
+        sums = (blank, blank, blank)
         if k == 0:
-            lax.fori_loop(0, GX // 2, outer_weights, 0)
             for side in range(2):
                 for held in (ohi, olo):
                     held[side, 1, 0, :TILE] = jnp.zeros((TILE, TILE), held.dtype)
-                    held[side, GX // 2, 1, 3 * TILE :] = jnp.zeros((TILE, TILE), held.dtype)
-        first, cross, square = outer(k, par)
+                    held[side, pairs, 1, 3 * TILE :] = jnp.zeros((TILE, TILE), held.dtype)
+
+            def both(p, carry):
+                outer_weights(p, 0)
+                return run(p - 2, carry)
+
+            lax.fori_loop(0, 2, outer_weights, 0)
+            sums = lax.fori_loop(2, pairs // 2 + 2, both, sums)
+            send_halo(1, 0)
+            sums = lax.fori_loop(pairs // 2 + 2, pairs, both, sums)
+            sums = lax.fori_loop(pairs - 2, pairs, run, sums, unroll=2)
+            send_halo(1, 1)
+        elif k == 1:
+            for part in range(2):
+                half = pairs // 2
+                sums = lax.fori_loop(part * half, (part + 1) * half, run, sums, unroll=half)
+                send_halo(2, part)
+        else:
+            sums = lax.fori_loop(0, pairs, run, sums, unroll=pairs)
+        first, cross, square = sums
         if k == 0:
             moments.append(first)
         if k < 2:
             moments += [cross, square]
-            send_halo(k + 1)
         else:
             moments.append((2.0 * GAIN * amp) * cross - amp * moments[4])
 
@@ -420,8 +452,19 @@
         for side in sends(k):
             @pl.when(has[side])
             def _(k=k, side=side):
-                for copy in copies(k, side):
-                    copy.wait_send()
+                for part in range(2):
+                    copy(k, side, part).wait_send()
+
+
+def ship(x_in, q_in, x_out, q_out, sem):
+    moves = [
+        pltpu.make_async_copy(source, held, sem.at[i])
+        for i, (source, held) in enumerate(((x_in, x_out), (q_in, q_out)))
+    ]
+    for move in moves:
+        move.start()
+    for move in moves:
+        move.wait()
 
 
 def shards(n, offsets, tile_cell, probes, target, lengthscale, amplitude, noise):
@@ -446,11 +489,9 @@
             pltpu.VMEM((1, local), F32),
             pltpu.VMEM((tiles, PAD, TILE), F32),
             pltpu.VMEM((3, GX, rows, PAD, TILE), F32),
-            pltpu.VMEM((3, rows, GX, 1, TILE), F32),
-            pltpu.VMEM((rows, GX, 2, TILE), F32),
             pltpu.VMEM((GX, rows, 2, TILE), F32),
-            pltpu.VMEM((3, 2, GX, RHS - 1, TILE), F32),
-            pltpu.VMEM((3, 2, GX, 1, TILE), F32),
+            pltpu.VMEM((3, 2, GX // CUT, CUT + 3, CUT, TILE), F32),
+            pltpu.VMEM((3, 2, GX // CUT, CUT + 3, CUT, TILE), F32),
             pltpu.VMEM((2, GX, 2, TILE), F32),
             pltpu.VMEM((2, GX + 2, 2 * PAD, wide), BF16),
             pltpu.VMEM((2, GX + 2, 2 * PAD, TILE), BF16),
@@ -465,8 +506,8 @@
             pltpu.VMEM((n, RHS - 1, TILE), F32),
             pltpu.SMEM((tiles,), jnp.int32),
             pltpu.SemaphoreType.DMA((4,)),
-            pltpu.SemaphoreType.DMA((3, 2, 3)),
-            pltpu.SemaphoreType.DMA((3, 2, 3)),
+            pltpu.SemaphoreType.DMA((3, 2, 2)),
+            pltpu.SemaphoreType.DMA((3, 2, 2)),
             pltpu.SemaphoreType.DMA((n,)),
             pltpu.SemaphoreType.DMA((n,)),
         ],
@@ -483,6 +524,19 @@
         amplitude,
         noise,
     )
+    hbm = pl.BlockSpec(memory_space=pltpu.HBM)
+    solutions, quadratic = pl.pallas_call(
+        ship,
+        out_shape=(
+            jax.ShapeDtypeStruct((RHS, local), F32),
+            jax.ShapeDtypeStruct((1, RHS), F32),
+        ),
+        in_specs=[vmem, vmem],
+        out_specs=(hbm, hbm),
+        scratch_shapes=[pltpu.SemaphoreType.DMA((2,))],
+        compiler_params=pltpu.CompilerParams(vmem_limit_bytes=4 * 1024 * 1024),
+        name="ship",
+    )(solutions, quadratic)
     return solutions, quadratic.reshape(RHS)
 
 

time: 31.9 us -> 30.6 us (0.959)
  local copies, waits for them, and re-layouts: 1.22 us -> 0 us
    unnamed x2 -> x0, local copies, waits for them, and re-layouts: 1.22 us -> none
    pallas_call x1, Pallas kernels: 27.9 us -> 27.1 us  [shards(): pl.pallas_call(functools.partial(kernel, n, rows, float(local * n)), out_...]
    pallas_call x0 -> x1, Pallas kernels: none -> 0.72 us  [shards(): pl.pallas_call(ship, out_shape=(jax.ShapeDtypeStruct((RHS, local), F32),...]
where the time goes in v3:
time: 30.6 us; the launch traced here: 30.4 us
  Pallas kernels  27.8 us (91%)
  between operations  2.58 us (8%)
    pallas_call x1, Pallas kernels, shards(): pl.pallas_call(functools.partial(kernel, n, rows, float(local * n)), out_...  27.1 us
    pallas_call x1, Pallas kernels, shards(): pl.pallas_call(ship, out_shape=(jax.ShapeDtypeStruct((RHS, local), F32),...  0.72 us

profile of v3, /device:TPU:0, one launch (start us, length us, event | category | flops | bytes accessed | tf_op | source)
XLA Modules:
  0.0 30.4 jit_solution(11451727373567552356)
XLA Ops:
  2.6 27.1 %solve.1 = (f32[9,4096]{1,0:T(8,128)S(1)}, f32[1,9]{1,0:T(1,128)S(1)}) custom-call(s32[32]{0:T(128)} %cell_in.1, f32[2,4096]{1,0:T(2,128)} %off_in.1, s32[8,4096]{1,0:T(8,128)} %probes_in.1, f32[1,4096]{1,0:T(1,128)} %bitcast.2, f32[1]{0:T(128)S(6)} %copy.9.length, f32[1]{0:T(128)S(6)} %copy.10.amp_ref, f32[1]{0:T(128)S(6)} %copy.11.noise_ref), custom_call_target="tpu_custom_call" | custom-call | tf_op jit(solution)/shard_map/solve/pallas_call | solution.py:476
  29.7 0.7 %ship.1 = (f32[9,4096]{1,0:T(8,128)}, f32[1,9]{1,0:T(1,128)}) custom-call(f32[9,4096]{1,0:T(8,128)S(1)} %get-tuple-element.6.x_in, f32[1,9]{1,0:T(1,128)S(1)} %get-tuple-element.7.q_in), custom_call_target="tpu_custom_call" | custom-call | tf_op jit(solution)/shard_map/ship/pallas_call | solution.py:528
